TPU v7x, 16 devices: a whole 2x2x2 slice. The times are simulated.
16 devices in a mesh: dp: 2 (over z), sp: 8 (over y, x, core).
Axes of the slice: x: 2, y: 2, z: 2, core: 2. Of those that a mesh axis runs over, the one named last changes fastest.
Arguments:
- x: bfloat16 [2, 4096, 3584], P('dp', 'sp'), parts along dimension 0
- segment_ids: int32 [2, 4096], P('dp', 'sp'), parts along dimension 0
- positions: int32 [2, 4096], P('dp', 'sp'), parts along dimension 0
- out_grad: bfloat16 [2, 4096, 3584], P('dp', 'sp'), parts along dimension 0
- norm_scale: bfloat16 [3584], replicated
- w_q: bfloat16 [3584, 4096], replicated
- w_k: bfloat16 [3584, 256], replicated
- w_v: bfloat16 [3584, 256], replicated
- w_o: bfloat16 [4096, 3584], replicated
- b_o: bfloat16 [3584], replicated
Outputs:
- output 1: bfloat16 [2, 4096, 3584], P('dp', 'sp'), parts along dimension 0
- output 2: bfloat16 [2, 4096, 3584], P('dp', 'sp'), parts along dimension 0
- output 3: bfloat16 [7168], P('dp'), parts along dimension 0
- output 4: bfloat16 [7168, 4096], P('dp'), parts along dimension 0
- output 5: bfloat16 [7168, 256], P('dp'), parts along dimension 0
- output 6: bfloat16 [7168, 256], P('dp'), parts along dimension 0
- output 7: bfloat16 [8192, 3584], P('dp'), parts along dimension 0
- output 8: bfloat16 [7168], P('dp'), parts along dimension 0
There are 2 independent parts. A program takes and returns all parts, laid end to end along the dimension named above; an argument that names none is the same for every part.
All inputs are finite; a program needn't handle non-finite values.
Results may differ from a plain program's by a relative error of at most 0.0176995.
Values are sent between devices in bfloat16 or wider.
A program may use at most 1 GiB of HBM per device.

v0:
```python
import jax
import jax.numpy as jnp
from jax import lax
from jax.experimental import pallas as pl
from jax.experimental.pallas import tpu as pltpu
from jax.sharding import PartitionSpec as P


WINDOW = 2048
NORM_EPS = 1e-6
ROPE_BASE = 10000.0
NEG_BIG = -1e30
HEAD_DIM = 256
Q_TILE = 256
K_TILE = 256
HEADS_PER_STEP = 2


def rms_norm(x_f32, gain_f32):
    mean_sq = jnp.mean(x_f32 * x_f32, axis=-1, keepdims=True)
    return (x_f32 * lax.rsqrt(mean_sq + NORM_EPS) * (1.0 + gain_f32)).astype(jnp.bfloat16)


def rotate(vals, cos2, sin2):
    low = vals[:, :128]
    swapped = jnp.concatenate([low[:, 64:], low[:, :64]], axis=1)
    return jnp.concatenate([low * cos2 + swapped * sin2, vals[:, 128:]], axis=1)


def nt_dot(a, b):
    return lax.dot_general(a, b, (((1,), (1,)), ((), ())), preferred_element_type=jnp.float32)


def nn_dot(a, b):
    return lax.dot_general(a, b, (((1,), (0,)), ((), ())), preferred_element_type=jnp.float32)


def attention_kernel(first_blk, base_blk, q_ref, do_ref, k_ref, v_ref, low_ref, cos_ref, sin_ref,
                     o_ref, dq_ref, dkv_ref,
                     cap, s_scr, dp_scr, q2, do2, q2t, do2t, m_acc, l_acc, d_acc, o_acc, dq_acc, dk_t, dv_t):
    q_idx, h_idx = pl.program_id(0), pl.program_id(1)
    rows = HEADS_PER_STEP * Q_TILE
    scale = HEAD_DIM ** -0.5
    kb_low = first_blk[q_idx]
    kb_end = q_idx + WINDOW // K_TILE + 1
    base = base_blk[0]

    @pl.when(jnp.logical_and(q_idx == 0, h_idx == 0))
    def _():
        dk_t[...] = jnp.zeros_like(dk_t)
        dv_t[...] = jnp.zeros_like(dv_t)

    @pl.when(h_idx == 0)
    def _():
        q_pos = WINDOW + q_idx * Q_TILE + lax.broadcasted_iota(jnp.int32, (Q_TILE, K_TILE), 0)
        low = low_ref[...]

        def fill(kb, _):
            k_pos = kb * K_TILE + lax.broadcasted_iota(jnp.int32, (Q_TILE, K_TILE), 1)
            allowed = jnp.logical_and(k_pos >= low, k_pos <= q_pos)
            cap[kb - q_idx] = jnp.where(allowed, jnp.inf, NEG_BIG)
            return 0

        lax.fori_loop(kb_low, kb_end, fill, 0)

    for h in range(HEADS_PER_STEP):
        cols = slice(h * HEAD_DIM, (h + 1) * HEAD_DIM)
        span = slice(h * Q_TILE, (h + 1) * Q_TILE)
        low_half = q_ref[:, h * HEAD_DIM:h * HEAD_DIM + 128]
        turned = low_half * cos_ref[...] + pltpu.roll(low_half, 64, 1) * sin_ref[...]
        q2[span, :128] = (turned * scale).astype(jnp.bfloat16)
        q2[span, 128:] = (q_ref[:, h * HEAD_DIM + 128:(h + 1) * HEAD_DIM] * scale).astype(jnp.bfloat16)
        do2[span, :] = do_ref[:, cols]
    q2t[...] = q2[...].T
    do2t[...] = do2[...].T

    m_acc[...] = jnp.full_like(m_acc, NEG_BIG)

    def scores(kb, _):
        keys = k_ref[pl.ds(pl.multiple_of((kb + base) * K_TILE, K_TILE), K_TILE), :]
        s = nt_dot(q2[...], keys)
        slot = kb - q_idx
        s = jnp.minimum(s.reshape(HEADS_PER_STEP, Q_TILE, K_TILE), cap[slot][None]).reshape(rows, K_TILE)
        s_scr[slot] = s
        m_acc[...] = jnp.maximum(m_acc[...], jnp.maximum(s[:, :128], s[:, 128:]))
        return 0

    lax.fori_loop(kb_low, kb_end, scores, 0)
    row_max = jnp.max(m_acc[...], axis=1, keepdims=True)
    m_acc[...] = jnp.broadcast_to(row_max, m_acc.shape)
    l_acc[...] = jnp.zeros_like(l_acc)
    d_acc[...] = jnp.zeros_like(d_acc)

    def exps(kb, _):
        vals = v_ref[pl.ds(pl.multiple_of((kb + base) * K_TILE, K_TILE), K_TILE), :]
        slot = kb - q_idx
        dp = nt_dot(do2[...], vals)
        m = m_acc[...]
        e0 = jnp.exp(s_scr[slot, :, :128] - m)
        e1 = jnp.exp(s_scr[slot, :, 128:] - m)
        s_scr[slot, :, :128] = e0
        s_scr[slot, :, 128:] = e1
        dp_scr[slot] = dp
        l_acc[...] += e0 + e1
        d_acc[...] += e0 * dp[:, :128] + e1 * dp[:, 128:]
        return 0

    lax.fori_loop(kb_low, kb_end, exps, 0)
    inv_l = 1.0 / jnp.sum(l_acc[...], axis=1, keepdims=True)
    delta = jnp.sum(d_acc[...], axis=1, keepdims=True) * inv_l
    l_acc[...] = jnp.broadcast_to(inv_l, l_acc.shape)
    d_acc[...] = jnp.broadcast_to(delta, d_acc.shape)
    o_acc[...] = jnp.zeros_like(o_acc)
    dq_acc[...] = jnp.zeros_like(dq_acc)

    def grads(kb, _):
        start = pl.multiple_of((kb + base) * K_TILE, K_TILE)
        keys = k_ref[pl.ds(start, K_TILE), :]
        vals = v_ref[pl.ds(start, K_TILE), :]
        slot = kb - q_idx
        inv = jnp.concatenate([l_acc[...], l_acc[...]], axis=1)
        dlt = jnp.concatenate([d_acc[...], d_acc[...]], axis=1)
        p = s_scr[slot] * inv
        ds = (p * (dp_scr[slot] - dlt)).astype(jnp.bfloat16)
        pb = p.astype(jnp.bfloat16)
        o_acc[...] += nn_dot(pb, vals)
        dq_acc[...] += nn_dot(ds, keys)
        dk_t[kb] += nn_dot(q2t[...], ds)
        dv_t[kb] += nn_dot(do2t[...], pb)
        return 0

    lax.fori_loop(kb_low, kb_end, grads, 0)

    for h in range(HEADS_PER_STEP):
        span = slice(h * Q_TILE, (h + 1) * Q_TILE)
        o_ref[:, h * HEAD_DIM:(h + 1) * HEAD_DIM] = o_acc[span, :].astype(jnp.bfloat16)
        dq = dq_acc[span, :].astype(jnp.bfloat16).astype(jnp.float32)
        low_half = dq[:, :128]
        turned = low_half * cos_ref[...] - pltpu.roll(low_half, 64, 1) * sin_ref[...]
        dq_ref[:, h * HEAD_DIM:h * HEAD_DIM + 128] = (turned * scale).astype(jnp.bfloat16)
        dq_ref[:, h * HEAD_DIM + 128:(h + 1) * HEAD_DIM] = (dq[:, 128:] * scale).astype(jnp.bfloat16)

    @pl.when(jnp.logical_and(q_idx == pl.num_programs(0) - 1, h_idx == pl.num_programs(1) - 1))
    def _():
        def flush(blk, _):
            rows_out = pl.ds(pl.multiple_of(blk * K_TILE, K_TILE), K_TILE)
            kb = blk - base
            inside = jnp.logical_and(kb >= 0, kb < dk_t.shape[0])

            @pl.when(inside)
            def _():
                dkv_ref[rows_out, :HEAD_DIM] = dk_t[kb].T
                dkv_ref[rows_out, HEAD_DIM:] = dv_t[kb].T

            @pl.when(jnp.logical_not(inside))
            def _():
                dkv_ref[rows_out, :] = jnp.zeros((K_TILE, 2 * HEAD_DIM), jnp.float32)

            return 0

        lax.fori_loop(0, dkv_ref.shape[0] // K_TILE, flush, 0)


def attention(q_lin, d_o, kv_all, low, base_blk, cos2, sin2):
    tokens, width = q_lin.shape
    span = kv_all.shape[0]
    n_q = tokens // Q_TILE
    step_cols = HEADS_PER_STEP * HEAD_DIM
    rows = HEADS_PER_STEP * Q_TILE
    slots = WINDOW // K_TILE + 1
    first_blk = low[::Q_TILE, 0] // K_TILE
    tile = pl.BlockSpec((Q_TILE, step_cols), lambda i, h, fb, bb: (i, h))
    k_spec = pl.BlockSpec((span, HEAD_DIM), lambda i, h, fb, bb: (0, 0))
    v_spec = pl.BlockSpec((span, HEAD_DIM), lambda i, h, fb, bb: (0, 1))
    local_blks = (WINDOW + tokens) // K_TILE
    side = pl.BlockSpec((Q_TILE, 128), lambda i, h, fb, bb: (i, 0))
    pairs = tokens * width // HEAD_DIM * WINDOW
    f32 = jnp.float32
    return pl.pallas_call(
        attention_kernel,
        out_shape=(jax.ShapeDtypeStruct((tokens, width), jnp.bfloat16),
                   jax.ShapeDtypeStruct((tokens, width), jnp.bfloat16),
                   jax.ShapeDtypeStruct((span, 2 * HEAD_DIM), f32)),
        grid_spec=pltpu.PrefetchScalarGridSpec(
            num_scalar_prefetch=2,
            grid=(n_q, width // step_cols),
            in_specs=[tile, tile, k_spec, v_spec, pl.BlockSpec((Q_TILE, 1), lambda i, h, fb, bb: (i, 0)), side, side],
            out_specs=[tile, tile, pl.BlockSpec((span, 2 * HEAD_DIM), lambda i, h, fb, bb: (0, 0))],
            scratch_shapes=[
                pltpu.VMEM((slots, Q_TILE, K_TILE), f32),
                pltpu.VMEM((slots, rows, K_TILE), f32),
                pltpu.VMEM((slots, rows, K_TILE), f32),
                pltpu.VMEM((rows, HEAD_DIM), jnp.bfloat16),
                pltpu.VMEM((rows, HEAD_DIM), jnp.bfloat16),
                pltpu.VMEM((HEAD_DIM, rows), jnp.bfloat16),
                pltpu.VMEM((HEAD_DIM, rows), jnp.bfloat16),
                pltpu.VMEM((rows, 128), f32),
                pltpu.VMEM((rows, 128), f32),
                pltpu.VMEM((rows, 128), f32),
                pltpu.VMEM((rows, HEAD_DIM), f32),
                pltpu.VMEM((rows, HEAD_DIM), f32),
                pltpu.VMEM((local_blks, HEAD_DIM, K_TILE), f32),
                pltpu.VMEM((local_blks, HEAD_DIM, K_TILE), f32),
            ]),
        compiler_params=pltpu.CompilerParams(
            dimension_semantics=("arbitrary", "arbitrary"), vmem_limit_bytes=60 * 1024 * 1024),
        cost_estimate=pl.CostEstimate(flops=12 * pairs * HEAD_DIM, bytes_accessed=32 * 1024 * 1024, transcendentals=pairs),
    )(first_blk, base_blk, q_lin, d_o, kv_all, kv_all, low, cos2, sin2)


def solution(mesh):
    row_spec = P("dp", "sp", None)
    tok_spec = P("dp", "sp")
    mat_spec = P(None, None)
    grad_mat = P("dp", None)
    n_sp = mesh.shape["sp"]
    f32, bf16 = jnp.float32, jnp.bfloat16

    def tn_dot(a, b):
        return lax.dot_general(a, b, (((0,), (0,)), ((), ())), preferred_element_type=f32).astype(bf16)

    def gather(a):
        return lax.all_gather(a, "sp", axis=0, tiled=True)

    def gather_chips(a):
        groups = [list(range(core, n_sp, 2)) for core in (0, 1)]
        return lax.all_gather(a, "sp", axis=0, tiled=True, axis_index_groups=groups)

    def swap(a, bit):
        return lax.ppermute(a, "sp", [(i, i ^ bit) for i in range(n_sp)])

    def tree_gather(a, me):
        rows = a.shape[0]
        half = rows // 2
        a_x, a_y, a_c = swap(a, 2), swap(a, 4), swap(a, 1)
        far = jnp.concatenate([swap(a_y[:half], 2), swap(a_x[half:], 4)], axis=0)
        mine = {0: a, 2: a_x, 4: a_y, 6: far}
        other = {0: a_c, 2: swap(a_x, 1), 4: swap(a_y, 1), 6: swap(far, 1)}
        out = jnp.zeros((n_sp * rows,) + a.shape[1:], a.dtype)
        for m, shard in mine.items():
            for bit, part in ((m, shard), (m ^ 1, other[m])):
                out = lax.dynamic_update_slice(out, part, ((me ^ bit) * rows,) + (0,) * (a.ndim - 1))
        return out

    def pair(core, own, got):
        out = jnp.zeros((2,) + own.shape, own.dtype)
        return put(put(out, own, core, 0), got, 1 - core, 0)

    def trade_halves(a, core):
        rows, half = a.shape[0], a.shape[1] // 2
        first, second = a[:, :half], a[:, half:]
        keep = jnp.where(core == 0, first, second)
        got = swap(jnp.where(core == 0, second, first), 1)
        return pair(core, keep, got).reshape(2 * rows, half)

    def tree_scatter_sum(a, me):
        rows = a.shape[0] // n_sp
        core, x_bit, y_bit = me & 1, (me >> 1) & 1, (me >> 2) & 1
        parts = a.reshape(n_sp // 2, 2, rows, a.shape[1])

        def pick(arr, idx, axis):
            return lax.dynamic_index_in_dim(arr, idx, axis, keepdims=False)

        got = swap(pick(parts, 1 - core, 1), 1)
        parts = pick(parts, core, 1) + got
        parts = parts.reshape(2, 2, rows, a.shape[1])
        half = rows // 2
        top, low = parts[:, :, :half], parts[:, :, half:]
        top = pick(top, x_bit, 1) + swap(pick(top, 1 - x_bit, 1), 2)
        low = pick(low, y_bit, 0) + swap(pick(low, 1 - y_bit, 0), 4)
        top = pick(top, y_bit, 0) + swap(pick(top, 1 - y_bit, 0), 4)
        low = pick(low, x_bit, 0) + swap(pick(low, 1 - x_bit, 0), 2)
        return jnp.concatenate([top, low], axis=0)

    def put(buf, part, core, col):
        return lax.dynamic_update_slice(buf, part[None], (core, 0, col))

    def step(x, seg_ids, positions, out_grad, norm_scale, w_q, w_k, w_v, w_o, b_o):
        tokens, width = x.shape[1], x.shape[2]
        heads_width = w_q.shape[1]
        me = lax.axis_index("sp")
        core = me & 1
        og = out_grad[0]
        og_all = gather(og)
        seg = seg_ids[0]
        seg_all = tree_gather(seg, me)

        x_f32 = x[0].astype(f32)
        normed, norm_pull = jax.vjp(rms_norm, x_f32, norm_scale.astype(f32))
        half = HEAD_DIM // 4
        inv_freq = ROPE_BASE ** (-(jnp.arange(half, dtype=f32) * 2.0 / (HEAD_DIM // 2)))
        angles = positions[0].astype(f32)[:, None] * inv_freq
        cos_a, sin_a = jnp.cos(angles), jnp.sin(angles)
        cos2 = jnp.concatenate([cos_a, cos_a], axis=1)
        sin2 = jnp.concatenate([-sin_a, sin_a], axis=1)

        keys = rotate(nn_dot(normed, w_k), cos2, sin2).astype(bf16)
        values = nn_dot(normed, w_v).astype(bf16)
        n_half = gather_chips(trade_halves(normed, core))
        kv_all = tree_gather(jnp.concatenate([keys, values], axis=1), me)

        base = me * tokens - WINDOW
        doc_start = jnp.sum((seg_all[None, :] < seg[:, None]).astype(jnp.int32), axis=1)
        low = jnp.maximum(doc_start - base, jnp.arange(tokens) + 1).astype(jnp.int32)[:, None]
        base_blk = (base // K_TILE).astype(jnp.int32).reshape(1)

        blanks = [jnp.ones(shape, bf16) for shape in ((2, heads_width // 2, width), (2, width // 2, heads_width))]
        *blanks, low = lax.optimization_barrier((*blanks, low))
        d_o = nt_dot(og, w_o).astype(bf16)
        q_lin = nn_dot(normed, w_q)
        o_tok, dq_lin, dkv_part = attention(q_lin, d_o, kv_all, low, base_blk, cos2, sin2)

        o_half = gather_chips(trade_halves(o_tok, core))
        cut = heads_width * 3 // 4
        dq_a = gather(dq_lin[:, :cut])
        dq_b = gather(dq_lin[:, cut:])

        block_out = (x_f32 + nn_dot(o_tok, w_o) + b_o.astype(f32)).astype(bf16)

        dkv = tree_scatter_sum(dkv_part, me).astype(bf16)
        dk_lin = rotate(dkv[:, :HEAD_DIM].astype(f32), cos2, -sin2).astype(bf16)
        dv_lin = dkv[:, HEAD_DIM:]
        dkv_all = tree_gather(jnp.concatenate([dk_lin, dv_lin], axis=1), me)

        d_normed = (nt_dot(dq_lin, w_q) + nt_dot(dk_lin, w_k) + nt_dot(dv_lin, w_v)).astype(bf16)
        dx_norm, gain_part = norm_pull(d_normed)
        x_grad = (og.astype(f32) + dx_norm).astype(bf16)
        small = jnp.stack([gain_part, jnp.sum(og, axis=0, dtype=f32)])
        for bit in (1, 2, 4):
            got = swap(small, bit)
            small = small + got
        small = small.astype(bf16)

        w_o_grad, w_q_grad = blanks

        def both(buf, part, col):
            got = swap(part, 1)
            return put(put(buf, part, core, col), got, 1 - core, col)

        o_rows = lax.optimization_barrier(tn_dot(o_half, og_all))
        w_o_grad = both(w_o_grad, o_rows, 0).reshape(heads_width, width)
        kv_rows = lax.optimization_barrier(tn_dot(n_half, dkv_all))
        w_kv_grad = pair(core, kv_rows, swap(kv_rows, 1)).reshape(width, 2 * HEAD_DIM)
        w_k_grad, w_v_grad = w_kv_grad[:, :HEAD_DIM], w_kv_grad[:, HEAD_DIM:]
        qa_rows = tn_dot(n_half, dq_a)
        w_q_grad = both(w_q_grad, qa_rows, 0)
        qb_rows = tn_dot(n_half, dq_b)
        w_q_grad = both(w_q_grad, qb_rows, cut).reshape(width, heads_width)
        return (block_out[None], x_grad[None], small[0], w_q_grad, w_k_grad, w_v_grad, w_o_grad, small[1])

    return jax.shard_map(step, mesh=mesh,
                         in_specs=(row_spec, tok_spec, tok_spec, row_spec, P(None), mat_spec, mat_spec, mat_spec, mat_spec, P(None)),
                         out_specs=(row_spec, row_spec, P("dp"), grad_mat, grad_mat, grad_mat, grad_mat, P("dp")),
                         check_vma=False)
```

profile of v0, /device:TPU:11, one launch (start us, length us, event | category | flops | bytes accessed | tf_op | source)
XLA Modules:
  0.0 922.9 jit_solution(10013875282043740207)
XLA Ops:
  7.2 3.0 fusion.10
  11.5 5.1 fusion.7
  16.6 3.5 broadcast_select_fusion.1
  20.7 2.1 broadcast_in_dim.73
  25.8 2.9 bitcast_dynamic-update-slice_fusion.10
  30.3 3.7 fusion.48
  36.3 3.9 convolution_convert_fusion.4
  44.4 23.6 %fusion.47.q_ref = f32[512,4096]{1,0:T(8,128)} fusion(bf16[512,3584]{1,0:T(8,128)(2,1)S(1)} %copy-done.3, bf16[3584,4096]{1,0:T(8,128)(2,1)} %param.15), kind=kOutput, calls=%fused_computation.137 | convolution fusion | flops 15032385536 | bytes 41418752 | tf_op jit(solution)/shard_map/dot_general | solution.py:35
  68.0 22.7 %convolution_convert_fusion.1.do_ref = bf16[512,4096]{1,0:T(8,128)(2,1)} fusion(bf16[4096,3584]{1,0:T(8,128)(2,1)} %param.18, bf16[1,512,3584]{2,1,0:T(8,128)(2,1)S(1)} %copy-done.7), kind=kOutput, calls=%fused_computation.29 | convolution fusion | flops 15034482688 | bytes 37224448 | tf_op jit(solution)/shard_map/dot_general | solution.py:31
  100.5 22.4 %collective-permute-done.11 = bf16[512,512]{1,0:T(8,128)(2,1)} collective-permute-done((bf16[512,512]{1,0:T(8,128)(2,1)}, bf16[512,512]{1,0:T(8,128)(2,1)}, u32[]{:S(2)}, u32[]{:S(2)}) %collective-permute-start.11) | collective-permute-done | bytes 524320 | tf_op jit(solution)/shard_map/ppermute | solution.py:230
  129.5 8.2 collective-permute-done.13
  146.9 64.0 %shard_map.161 = (bf16[512,4096]{1,0:T(8,128)(2,1)}, bf16[512,4096]{1,0:T(8,128)(2,1)}, f32[4096,512]{1,0:T(8,128)}) custom-call(s32[2]{0:T(128)} %and_select_fusion.first_blk, s32[1]{0:T(128)} %bitcast.3.base_blk, f32[512,4096]{1,0:T(8,128)} %fusion.47.q_ref, bf16[512,4096]{1,0:T(8,128)(2,1)} %convolution_convert_fusion.1.do_ref, ...), custom_call_target="tpu_custom_call" | custom-call | flops 51539607552 | bytes 33554432 | tf_op jit(solution)/shard_map/pallas_call | solution.py:179
  210.9 3.8 slice.117
  214.7 2.6 broadcast_select_fusion
  217.4 2.5 broadcast_in_dim.83
  219.9 2.1 bitcast_dynamic-update-slice_fusion.7
  224.1 4.7 dynamic-slice_bitcast_fusion
  229.3 7.1 collective-permute-done.16
  236.4 4.5 bitcast_add_fusion
  245.0 65.1 %collective-permute-start.19 = (f32[2,256,512]{2,1,0:T(8,128)}, f32[2,256,512]{2,1,0:T(8,128)}, u32[]{:S(2)}, u32[]{:S(2)}) collective-permute-start(f32[2,256,512]{2,1,0:T(8,128)} %dynamic-slice_bitcast_fusion.1), channel_id=1, source_target_pairs={{0,4},{1,5},{2,6},{3,7},{4,0},{5,1},{6,2},{7,3},{8,12},{9,13},{10,... | collective-permute-start | bytes 3145736 | tf_op jit(solution)/shard_map/ppermute | solution.py:230
  310.1 2.3 dynamic-slice_bitcast_fusion.2
  312.4 34.1 %collective-permute-done.19 = f32[2,256,512]{2,1,0:T(8,128)} collective-permute-done((f32[2,256,512]{2,1,0:T(8,128)}, f32[2,256,512]{2,1,0:T(8,128)}, u32[]{:S(2)}, u32[]{:S(2)}) %collective-permute-start.19) | collective-permute-done | bytes 1048608 | tf_op jit(solution)/shard_map/ppermute | solution.py:230
  350.1 18.6 %collective-permute-done.20 = f32[256,512]{1,0:T(8,128)S(1)} collective-permute-done((f32[256,512]{1,0:T(8,128)S(1)}, f32[256,512]{1,0:T(8,128)S(1)}, u32[]{:S(2)}, u32[]{:S(2)}) %collective-permute-start.20) | collective-permute-done | bytes 524320 | tf_op jit(solution)/shard_map/ppermute | solution.py:230
  368.8 2.1 collective-permute-done.18
  371.5 4.2 fusion.24
  375.7 4.2 fusion.32
  380.0 27.3 %fusion.9 = (f32[3584]{0:T(1024)S(1)}, f32[512]{0:T(512)S(1)}, bf16[512,3584]{1,0:T(8,128)(2,1)}) fusion(bf16[1,512,3584]{2,1,0:T(8,128)(2,1)S(1)} %copy-done.4, f32[512]{0:T(512)S(1)} %copy-done.20, f32[3584]{0:T(1024)S(1)} %copy-done.16, f32[512,3584]{1,0:T(8,128)} %fusion.24, f32[512,3584]{1,0:T(8,128)} %fusion.32, ...), kind=kOutput, calls=%fused_computation.23 | convolution fusion | flops 15052566528 | bytes 55607296 | tf_op jit(solution)/shard_map/dot_general | solution.py:31
  407.3 6.4 convert_reduce_fusion
  413.7 2.9 collective-permute-start.21
  419.2 2.6 collective-permute-start.28
  422.0 2.3 slice.118
  424.9 17.5 %collective-permute-done.30 = bf16[512,512]{1,0:T(8,128)(2,1)S(1)} collective-permute-done((bf16[512,512]{1,0:T(8,128)(2,1)S(1)}, bf16[512,512]{1,0:T(8,128)(2,1)S(1)}, u32[]{:S(2)}, u32[]{:S(2)}) %collective-permute-start.30) | collective-permute-done | bytes 524320 | tf_op jit(solution)/shard_map/ppermute | solution.py:230
  458.0 14.0 %convolution_convert_fusion.3 = bf16[1792,512]{1,0:T(8,128)(2,1)} fusion(bf16[4096,1792]{1,0:T(8,128)(2,1)} %all-gather.7.cloned.1.call-done, bf16[4096,512]{1,0:T(8,128)(2,1)} %constant_dynamic-update-slice_fusion.5), kind=kOutput, calls=%fused_computation.38 | convolution fusion | flops 7517110272 | bytes 20709376 | tf_op jit(solution)/shard_map/dot_general | solution.py:220
  472.2 14.0 %broadcast_in_dim.69 = bf16[2,1792,4096]{2,1,0:T(8,128)(2,1)} broadcast(bf16[]{:T(256)} %constant.103.clone.1), dimensions={} | broadcast | bytes 29360130 | tf_op jit(solution)/shard_map/broadcast_in_dim | solution.py:307
  486.6 52.5 %bitcast_dynamic-update-slice_fusion.3 = (bf16[2,1792,4096]{2,1,0:T(8,128)(2,1)}, bf16[1792,3072]{1,0:T(8,128)(2,1)}) fusion(bf16[2,1792,4096]{2,1,0:T(8,128)(2,1)} %broadcast_in_dim.69, s32[]{:T(128)S(6)} %select_n.122, bf16[4096,1792]{1,0:T(8,128)(2,1)S(1)} %copy-done.24, bf16[4096,3072]{1,0:T(8,128)(2,1)} %all-gather.9.cloned.1.call-done), kind=kOutput, calls=%fused_computation.12 | convolution fusion | flops 45102661632 | bytes 61865988 | tf_op jit(solution)/shard_map/dot_general | solution.py:220
  539.5 59.1 %all-gather.13.cloned.1.call-done = bf16[4096,2048]{1,0:T(8,128)(2,1)} async-done(((bf16[1024,2048]{1,0:T(8,128)(2,1)}), bf16[4096,2048]{1,0:T(8,128)(2,1)}) %all-gather.13.cloned.1.call-update) | async-done | bytes 16777232 | tf_op jit(solution)/shard_map/all_gather | solution.py:227
  598.6 141.5 %all-gather.15.cloned.1.call-done = bf16[1,4096,3584]{2,1,0:T(8,128)(2,1)} async-done(((bf16[1,512,3584]{2,1,0:T(8,128)(2,1)}), bf16[1,4096,3584]{2,1,0:T(8,128)(2,1)}) %all-gather.15.cloned.1.call-update) | async-done | bytes 29360144 | tf_op jit(solution)/shard_map/all_gather | solution.py:223
  740.1 71.4 %fusion.2 = bf16[2048,3584]{1,0:T(8,128)(2,1)} fusion(bf16[4096,2048]{1,0:T(8,128)(2,1)} %all-gather.13.cloned.1.call-done, bf16[1,4096,3584]{2,1,0:T(8,128)(2,1)} %all-gather.15.cloned.1.call-done), kind=kOutput, calls=%fused_computation.2 | convolution fusion | flops 60136882176 | bytes 60817408 | tf_op jit(solution)/shard_map/dot_general | solution.py:220
  811.7 23.3 %fusion.14 = bf16[1,512,3584]{2,1,0:T(8,128)(2,1)} fusion(bf16[512,4096]{1,0:T(8,128)(2,1)} %get-tuple-element.15, bf16[4096,3584]{1,0:T(8,128)(2,1)} %param.18, bf16[1,512,3584]{2,1,0:T(8,128)(2,1)S(1)} %copy-done.5, f32[3584]{0:T(1024)S(1)} %convert_element_type.80), kind=kOutput, calls=%fused_computation.30 | convolution fusion | flops 15039725568 | bytes 40908800 | tf_op jit(solution)/shard_map/dot_general | solution.py:35
  838.6 2.9 bitcast_dynamic-update-slice_fusion.9
  841.4 2.9 bitcast_dynamic-update-slice_fusion.8
  844.3 10.1 %bitcast_dynamic-update-slice_fusion.2 = bf16[2,1792,4096]{2,1,0:T(8,128)(2,1)} fusion(bf16[2,1792,4096]{2,1,0:T(8,128)(2,1)} %get-tuple-element.45, s32[]{:T(128)S(6)} %select_n.123, bf16[1792,3072]{1,0:T(8,128)(2,1)} %collective-permute-done.25), kind=kLoop, calls=%fused_computation.11 | loop fusion | bytes 22020100 | tf_op jit(solution)/shard_map/dynamic_update_slice | solution.py:276
  854.4 23.2 %bitcast_dynamic-update-slice_fusion.5 = (bf16[2,1792,4096]{2,1,0:T(8,128)(2,1)}, bf16[1792,1024]{1,0:T(8,128)(2,1)}) fusion(bf16[2,1792,4096]{2,1,0:T(8,128)(2,1)} %bitcast_dynamic-update-slice_fusion.2, s32[]{:T(128)S(6)} %select_n.122, bf16[4096,1792]{1,0:T(8,128)(2,1)} %all-gather.7.cloned.1.call-done, bf16[4096,1024]{1,0:T(8,128)(2,1)} %all-gather.11.cloned.1.call-done), kind=kOutput, calls=%fused_computation.36 | convolution fusion | flops 15034220544 | bytes 30408708 | tf_op jit(solution)/shard_map/dot_general | solution.py:220
  877.9 4.3 fusion.44
  882.1 12.6 %broadcast_in_dim.68 = bf16[2,2048,3584]{2,1,0:T(8,128)(2,1)} broadcast(bf16[]{:T(256)} %constant.103.clone.1), dimensions={} | broadcast | bytes 29360130 | tf_op jit(solution)/shard_map/broadcast_in_dim | solution.py:307
  894.8 5.9 bitcast_dynamic-update-slice_fusion.1
  900.7 2.2 bitcast_dynamic-update-slice_fusion.4
  902.9 13.2 %bitcast_dynamic-update-slice_fusion = bf16[2,2048,3584]{2,1,0:T(8,128)(2,1)} fusion(bf16[2,2048,3584]{2,1,0:T(8,128)(2,1)} %bitcast_dynamic-update-slice_fusion.1, s32[]{:T(128)S(6)} %select_n.123, bf16[2048,3584]{1,0:T(8,128)(2,1)} %collective-permute-done.37), kind=kLoop, calls=%fused_computation.3 | loop fusion | bytes 29360132 | tf_op jit(solution)/shard_map/dynamic_update_slice | solution.py:276
  (217 shorter events, 73.3 us)
Async XLA Ops:
  7.2 29.1 %copy-start = (bf16[3584,256]{1,0:T(8,128)(2,1)S(1)}, bf16[3584,256]{1,0:T(8,128)(2,1)}, u32[]{:S(2)}) copy-start(bf16[3584,256]{1,0:T(8,128)(2,1)} %param.17) | copy-start | bytes 5505028
  7.2 450.8 %all-gather.7.cloned.1.call-start = ((), (), s32[]{:S(2)}) async-start(), calls=%async_computation | async-start | bytes 18350080 | tf_op jit(solution)/shard_map/all_gather | solution.py:227
  20.1 5.7 collective-permute-start.24
  28.7 443.5 %all-gather.9.cloned.1.call-start = ((), (), s32[]{:S(2)}) async-start(), calls=%async_computation.1 | async-start | bytes 28311552 | tf_op jit(solution)/shard_map/all_gather | solution.py:223
  28.7 67.9 %collective-permute-start = (s32[512]{0:T(512)S(1)}, s32[512]{0:T(512)S(1)}, u32[]{:S(2)}, u32[]{:S(2)}) collective-permute-start(s32[512]{0:T(512)S(1)} %bitcast.110), channel_id=1, source_target_pairs={{0,1},{1,0},{2,3},{3,2},{4,5},{5,4},{6,7},{7,6},{8,9},{9,8},{10,11... | collective-permute-start | bytes 6152 | tf_op jit(solution)/shard_map/ppermute | solution.py:230
  28.8 63.0 %collective-permute-start.1 = (s32[512]{0:T(512)S(1)}, s32[512]{0:T(512)S(1)}, u32[]{:S(2)}, u32[]{:S(2)}) collective-permute-start(s32[512]{0:T(512)S(1)} %bitcast.111), channel_id=1, source_target_pairs={{0,2},{1,3},{2,0},{3,1},{4,6},{5,7},{6,4},{7,5},{8,10},{9,11},{10,... | collective-permute-start | bytes 6152 | tf_op jit(solution)/shard_map/ppermute | solution.py:230
  29.1 61.6 %collective-permute-start.3 = (s32[512]{0:T(512)S(1)}, s32[512]{0:T(512)S(1)}, u32[]{:S(2)}, u32[]{:S(2)}) collective-permute-start(s32[512]{0:T(512)S(1)} %bitcast.112), channel_id=1, source_target_pairs={{0,4},{1,5},{2,6},{3,7},{4,0},{5,1},{6,2},{7,3},{8,12},{9,13},{10,... | collective-permute-start | bytes 6152 | tf_op jit(solution)/shard_map/ppermute | solution.py:230
  43.5 84.1 %collective-permute-start.8 = (bf16[512,512]{1,0:T(8,128)(2,1)}, bf16[512,512]{1,0:T(8,128)(2,1)}, u32[]{:S(2)}, u32[]{:S(2)}) collective-permute-start(bf16[512,512]{1,0:T(8,128)(2,1)} %get-tuple-element.36), channel_id=1, source_target_pairs={{0,1},{1,0},{2,3},{3,2},{4,5},{5,4},{6,7},{7,6},{8,9},{9,8},{10,11... | collective-permute-start | bytes 1572872 | tf_op jit(solution)/shard_map/ppermute | solution.py:230
  90.6 3.0 collective-permute-start.5
  91.8 3.3 collective-permute-start.6
  92.1 5.5 collective-permute-start.2
  93.6 4.7 collective-permute-start.4
  95.1 3.6 collective-permute-start.7
  96.6 28.3 %collective-permute-start.9 = (bf16[512,512]{1,0:T(8,128)(2,1)}, bf16[512,512]{1,0:T(8,128)(2,1)S(1)}, u32[]{:S(2)}, u32[]{:S(2)}) collective-permute-start(bf16[512,512]{1,0:T(8,128)(2,1)} %get-tuple-element.36), channel_id=1, source_target_pairs={{0,2},{1,3},{2,0},{3,1},{4,6},{5,7},{6,4},{7,5},{8,10},{9,11},{10,... | collective-permute-start | bytes 1572872 | tf_op jit(solution)/shard_map/ppermute | solution.py:230
  97.6 25.4 %collective-permute-start.11 = (bf16[512,512]{1,0:T(8,128)(2,1)}, bf16[512,512]{1,0:T(8,128)(2,1)}, u32[]{:S(2)}, u32[]{:S(2)}) collective-permute-start(bf16[512,512]{1,0:T(8,128)(2,1)} %get-tuple-element.36), channel_id=1, source_target_pairs={{0,4},{1,5},{2,6},{3,7},{4,0},{5,1},{6,2},{7,3},{8,12},{9,13},{10,... | collective-permute-start | bytes 1572872 | tf_op jit(solution)/shard_map/ppermute | solution.py:230
  100.4 45.6 %copy-start.14 = (s32[512,1]{1,0:T(8,128)}, s32[512,1]{1,0:T(8,128)S(1)}, u32[]{:S(2)}) copy-start(s32[512,1]{1,0:T(8,128)S(1)} %add_maximum_fusion.low_ref) | copy-start | bytes 6148
  124.0 13.7 %collective-permute-start.13 = (bf16[256,512]{1,0:T(8,128)(2,1)S(1)}, bf16[256,512]{1,0:T(8,128)(2,1)S(1)}, u32[]{:S(2)}, u32[]{:S(2)}) collective-permute-start(bf16[256,512]{1,0:T(8,128)(2,1)S(1)} %slice.131), channel_id=1, source_target_pairs={{0,2},{1,3},{2,0},{3,1},{4,6},{5,7},{6,4},{7,5},{8,10},{9,11},{10,... | collective-permute-start | bytes 786440 | tf_op jit(solution)/shard_map/ppermute | solution.py:230
  125.0 13.6 %collective-permute-start.14 = (bf16[256,512]{1,0:T(8,128)(2,1)S(1)}, bf16[256,512]{1,0:T(8,128)(2,1)S(1)}, u32[]{:S(2)}, u32[]{:S(2)}) collective-permute-start(bf16[256,512]{1,0:T(8,128)(2,1)S(1)} %slice.132), channel_id=1, source_target_pairs={{0,4},{1,5},{2,6},{3,7},{4,0},{5,1},{6,2},{7,3},{8,12},{9,13},{10,... | collective-permute-start | bytes 786440 | tf_op jit(solution)/shard_map/ppermute | solution.py:230
  125.4 16.1 %collective-permute-start.10 = (bf16[512,512]{1,0:T(8,128)(2,1)S(1)}, bf16[512,512]{1,0:T(8,128)(2,1)S(1)}, u32[]{:S(2)}, u32[]{:S(2)}) collective-permute-start(bf16[512,512]{1,0:T(8,128)(2,1)S(1)} %collective-permute-done.9), channel_id=1, source_target_pairs={{0,1},{1,0},{2,3},{3,2},{4,5},{5,4},{6,7},{7,6},{8,9},{9,8},{10,11... | collective-permute-start | bytes 1572872 | tf_op jit(solution)/shard_map/ppermute | solution.py:230
  127.6 16.7 %collective-permute-start.12 = (bf16[512,512]{1,0:T(8,128)(2,1)}, bf16[512,512]{1,0:T(8,128)(2,1)S(1)}, u32[]{:S(2)}, u32[]{:S(2)}) collective-permute-start(bf16[512,512]{1,0:T(8,128)(2,1)} %collective-permute-done.11), channel_id=1, source_target_pairs={{0,1},{1,0},{2,3},{3,2},{4,5},{5,4},{6,7},{7,6},{8,9},{9,8},{10,11... | collective-permute-start | bytes 1572872 | tf_op jit(solution)/shard_map/ppermute | solution.py:230
  138.7 7.4 collective-permute-start.15
  214.7 384.0 %all-gather.13.cloned.1.call-start = ((), (), s32[]{:S(2)}) async-start(), calls=%async_computation.3 | async-start | bytes 20971520 | tf_op jit(solution)/shard_map/all_gather | solution.py:227
  217.3 4.7 collective-permute-start.36
  223.5 516.6 %all-gather.15.cloned.1.call-start = ((), (), s32[]{:S(2)}) async-start(), calls=%async_computation.4 | async-start | bytes 33030144 | tf_op jit(solution)/shard_map/all_gather | solution.py:223
  224.1 630.3 %all-gather.11.cloned.1.call-start = ((), (), s32[]{:S(2)}) async-start(), calls=%async_computation.2 | async-start | bytes 9437184 | tf_op jit(solution)/shard_map/all_gather | solution.py:223
  228.8 7.6 collective-permute-start.16
  245.0 101.5 %collective-permute-start.19 = (f32[2,256,512]{2,1,0:T(8,128)}, f32[2,256,512]{2,1,0:T(8,128)}, u32[]{:S(2)}, u32[]{:S(2)}) collective-permute-start(f32[2,256,512]{2,1,0:T(8,128)} %dynamic-slice_bitcast_fusion.1), channel_id=1, source_target_pairs={{0,4},{1,5},{2,6},{3,7},{4,0},{5,1},{6,2},{7,3},{8,12},{9,13},{10,... | collective-permute-start | bytes 3145736 | tf_op jit(solution)/shard_map/ppermute | solution.py:230
  312.3 36.0 %collective-permute-start.17 = (f32[2,256,512]{2,1,0:T(8,128)}, f32[2,256,512]{2,1,0:T(8,128)}, u32[]{:S(2)}, u32[]{:S(2)}) collective-permute-start(f32[2,256,512]{2,1,0:T(8,128)} %dynamic-slice_bitcast_fusion.2), channel_id=1, source_target_pairs={{0,2},{1,3},{2,0},{3,1},{4,6},{5,7},{6,4},{7,5},{8,10},{9,11},{10,... | collective-permute-start | bytes 3145736 | tf_op jit(solution)/shard_map/ppermute | solution.py:230
  312.4 36.0 %copy-start.8 = (f32[2,2,256,512]{3,2,1,0:T(8,128)S(1)}, f32[2,2,256,512]{3,2,1,0:T(8,128)}, u32[]{:S(2)}) copy-start(f32[2,2,256,512]{3,2,1,0:T(8,128)} %get-tuple-element.29) | copy-start | bytes 6291460
  348.3 20.4 %collective-permute-start.20 = (f32[256,512]{1,0:T(8,128)S(1)}, f32[256,512]{1,0:T(8,128)S(1)}, u32[]{:S(2)}, u32[]{:S(2)}) collective-permute-start(f32[256,512]{1,0:T(8,128)S(1)} %dynamic-slice_bitcast_fusion.3), channel_id=1, source_target_pairs={{0,2},{1,3},{2,0},{3,1},{4,6},{5,7},{6,4},{7,5},{8,10},{9,11},{10,... | collective-permute-start | bytes 1572872 | tf_op jit(solution)/shard_map/ppermute | solution.py:230
  349.9 21.1 %collective-permute-start.18 = (f32[256,512]{1,0:T(8,128)S(1)}, f32[256,512]{1,0:T(8,128)S(1)}, u32[]{:S(2)}, u32[]{:S(2)}) collective-permute-start(f32[256,512]{1,0:T(8,128)S(1)} %dynamic-slice_bitcast_fusion.4), channel_id=1, source_target_pairs={{0,4},{1,5},{2,6},{3,7},{4,0},{5,1},{6,2},{7,3},{8,12},{9,13},{10,... | collective-permute-start | bytes 1572872 | tf_op jit(solution)/shard_map/ppermute | solution.py:230
  379.9 27.3 %copy-start.18 = (f32[512]{0:T(512)S(1)}, f32[512]{0:T(512)}, u32[]{:S(2)}) copy-start(f32[512]{0:T(512)} %copy-done.17) | copy-start | bytes 6148
  413.7 8.2 collective-permute-start.21
  419.1 23.3 %collective-permute-start.30 = (bf16[512,512]{1,0:T(8,128)(2,1)S(1)}, bf16[512,512]{1,0:T(8,128)(2,1)S(1)}, u32[]{:S(2)}, u32[]{:S(2)}) collective-permute-start(bf16[512,512]{1,0:T(8,128)(2,1)S(1)} %get-tuple-element.25), channel_id=1, source_target_pairs={{0,4},{1,5},{2,6},{3,7},{4,0},{5,1},{6,2},{7,3},{8,12},{9,13},{10,... | collective-permute-start | bytes 1572872 | tf_op jit(solution)/shard_map/ppermute | solution.py:230
  419.2 24.6 %collective-permute-start.28 = (bf16[512,512]{1,0:T(8,128)(2,1)S(1)}, bf16[512,512]{1,0:T(8,128)(2,1)S(1)}, u32[]{:S(2)}, u32[]{:S(2)}) collective-permute-start(bf16[512,512]{1,0:T(8,128)(2,1)S(1)} %get-tuple-element.25), channel_id=1, source_target_pairs={{0,2},{1,3},{2,0},{3,1},{4,6},{5,7},{6,4},{7,5},{8,10},{9,11},{10,... | collective-permute-start | bytes 1572872 | tf_op jit(solution)/shard_map/ppermute | solution.py:230
  421.9 23.3 %collective-permute-start.22 = (f32[2,3584]{1,0:T(2,128)S(1)}, f32[2,3584]{1,0:T(2,128)S(1)}, u32[]{:S(2)}, u32[]{:S(2)}) collective-permute-start(f32[2,3584]{1,0:T(2,128)S(1)} %fusion.41), channel_id=1, source_target_pairs={{0,2},{1,3},{2,0},{3,1},{4,6},{5,7},{6,4},{7,5},{8,10},{9,11},{10,... | collective-permute-start | bytes 86024 | tf_op jit(solution)/shard_map/ppermute | solution.py:230
  424.3 22.9 %collective-permute-start.27 = (bf16[512,512]{1,0:T(8,128)(2,1)S(1)}, bf16[512,512]{1,0:T(8,128)(2,1)S(1)}, u32[]{:S(2)}, u32[]{:S(2)}) collective-permute-start(bf16[512,512]{1,0:T(8,128)(2,1)S(1)} %get-tuple-element.25), channel_id=1, source_target_pairs={{0,1},{1,0},{2,3},{3,2},{4,5},{5,4},{6,7},{7,6},{8,9},{9,8},{10,11... | collective-permute-start | bytes 1572872 | tf_op jit(solution)/shard_map/ppermute | solution.py:230
  442.4 7.4 collective-permute-start.32
  443.9 7.1 collective-permute-start.33
  444.1 9.7 %collective-permute-start.29 = (bf16[512,512]{1,0:T(8,128)(2,1)S(1)}, bf16[512,512]{1,0:T(8,128)(2,1)S(1)}, u32[]{:S(2)}, u32[]{:S(2)}) collective-permute-start(bf16[512,512]{1,0:T(8,128)(2,1)S(1)} %collective-permute-done.28), channel_id=1, source_target_pairs={{0,1},{1,0},{2,3},{3,2},{4,5},{5,4},{6,7},{7,6},{8,9},{9,8},{10,11... | collective-permute-start | bytes 1572872 | tf_op jit(solution)/shard_map/ppermute | solution.py:230
  445.9 389.2 %collective-permute-start.23 = (f32[2,3584]{1,0:T(2,128)}, f32[2,3584]{1,0:T(2,128)}, u32[]{:S(2)}, u32[]{:S(2)}) collective-permute-start(f32[2,3584]{1,0:T(2,128)} %fusion.69), channel_id=1, source_target_pairs={{0,4},{1,5},{2,6},{3,7},{4,0},{5,1},{6,2},{7,3},{8,12},{9,13},{10,... | collective-permute-start | bytes 86024 | tf_op jit(solution)/shard_map/ppermute | solution.py:230
  447.1 8.4 collective-permute-start.31
  451.0 6.1 collective-permute-start.34
  472.0 369.4 %collective-permute-start.35 = (bf16[1792,512]{1,0:T(8,128)(2,1)}, bf16[1792,512]{1,0:T(8,128)(2,1)}, u32[]{:S(2)}, u32[]{:S(2)}) collective-permute-start(bf16[1792,512]{1,0:T(8,128)(2,1)} %convolution_convert_fusion.3), channel_id=1, source_target_pairs={{0,1},{1,0},{2,3},{3,2},{4,5},{5,4},{6,7},{7,6},{8,9},{9,8},{10,11... | collective-permute-start | bytes 5505032 | tf_op jit(solution)/shard_map/ppermute | solution.py:230
  539.1 305.2 %collective-permute-start.25 = (bf16[1792,3072]{1,0:T(8,128)(2,1)}, bf16[1792,3072]{1,0:T(8,128)(2,1)}, u32[]{:S(2)}, u32[]{:S(2)}) collective-permute-start(bf16[1792,3072]{1,0:T(8,128)(2,1)} %get-tuple-element.46), channel_id=1, source_target_pairs={{0,1},{1,0},{2,3},{3,2},{4,5},{5,4},{6,7},{7,6},{8,9},{9,8},{10,11... | collective-permute-start | bytes 33030152 | tf_op jit(solution)/shard_map/ppermute | solution.py:230
  740.1 71.6 %copy-start.5 = (bf16[1,512,3584]{2,1,0:T(8,128)(2,1)S(1)}, bf16[1,512,3584]{2,1,0:T(8,128)(2,1)}, u32[]{:S(2)}) copy-start(bf16[1,512,3584]{2,1,0:T(8,128)(2,1)} %param.10) | copy-start | bytes 11010052
  811.5 91.4 %collective-permute-start.37 = (bf16[2048,3584]{1,0:T(8,128)(2,1)}, bf16[2048,3584]{1,0:T(8,128)(2,1)}, u32[]{:S(2)}, u32[]{:S(2)}) collective-permute-start(bf16[2048,3584]{1,0:T(8,128)(2,1)} %fusion.2), channel_id=1, source_target_pairs={{0,1},{1,0},{2,3},{3,2},{4,5},{5,4},{6,7},{7,6},{8,9},{9,8},{10,11... | collective-permute-start | bytes 44040200 | tf_op jit(solution)/shard_map/ppermute | solution.py:230
  877.6 23.1 %collective-permute-start.26 = (bf16[1792,1024]{1,0:T(8,128)(2,1)}, bf16[1792,1024]{1,0:T(8,128)(2,1)S(1)}, u32[]{:S(2)}, u32[]{:S(2)}) collective-permute-start(bf16[1792,1024]{1,0:T(8,128)(2,1)} %get-tuple-element.48), channel_id=1, source_target_pairs={{0,1},{1,0},{2,3},{3,2},{4,5},{5,4},{6,7},{7,6},{8,9},{9,8},{10,11... | collective-permute-start | bytes 11010056 | tf_op jit(solution)/shard_map/ppermute | solution.py:230
  (24 other events, 199.2 us)
Sparse Core Ops, SparseCore 0:
  28.8 153.2 all-gather.6
  214.8 228.9 all-gather.8
  445.6 152.9 all-gather.12
  600.3 139.7 all-gather.14
  742.4 50.4 all-gather.10
where the time goes:
time: 931 us; the launch traced here: 923 us
  waiting for transfers between devices  315 us (34%)
  matrix products  274 us (29%)
  local copies, waits for them, and re-layouts  121 us (13%)
  starting transfers between devices  94.5 us (10%)
  Pallas kernels  64 us (7%)
  other arithmetic  39.4 us (4%)
  between operations  14.5 us (2%)
    dot_general x4, matrix products, tn_dot(): lax.dot_general(a, b, (((0,), (0,)), ((), ())), preferred_element_type=f32)  161 us
    all_gather x3, waiting for transfers between devices, gather(): return lax.all_gather(a, 'sp', axis=0, tiled=True)  141 us
    ppermute x38, waiting for transfers between devices, swap(): return lax.ppermute(a, 'sp', [(i, i ^ bit) for i in range(n_sp)])  114 us
    ppermute x38, starting transfers between devices, swap(): return lax.ppermute(a, 'sp', [(i, i ^ bit) for i in range(n_sp)])  94.3 us
    pallas_call x1, Pallas kernels, attention(): pl.pallas_call(attention_kernel, out_shape=(jax.ShapeDtypeStruct((tokens,...  64 us
    all_gather x2, waiting for transfers between devices, gather_chips(): return lax.all_gather(a, 'sp', axis=0, tiled=True, axis_index_groups=groups)  59.1 us
    dot_general x4, matrix products, nt_dot(): lax.dot_general(a, b, (((1,), (1,)), ((), ())), preferred_element_type=jn...  58.4 us
    dot_general x4, matrix products, nn_dot(): lax.dot_general(a, b, (((1,), (0,)), ((), ())), preferred_element_type=jn...  54.5 us
  transfers between devices with their start and end apart: 43, of which 13 were waited for; matrix products, arithmetic and copies ran while one was open for 43% of the time, Pallas kernels for 7%

commit v1 on v0

--- a/solution.py
+++ b/solution.py
@@ -334,8 +334,8 @@
         w_o_grad, w_q_grad = blanks
 
         def both(buf, part, col):
-            got = swap(part, 1)
-            return put(put(buf, part, core, col), got, 1 - core, col)
+            buf = put(buf, part, core, col)
+            return put(buf, swap(part, 1), 1 - core, col)
 
         o_rows = lax.optimization_barrier(tn_dot(o_half, og_all))
         w_o_grad = both(w_o_grad, o_rows, 0).reshape(heads_width, width)
@@ -343,9 +343,11 @@
         w_kv_grad = pair(core, kv_rows, swap(kv_rows, 1)).reshape(width, 2 * HEAD_DIM)
         w_k_grad, w_v_grad = w_kv_grad[:, :HEAD_DIM], w_kv_grad[:, HEAD_DIM:]
         qa_rows = tn_dot(n_half, dq_a)
-        w_q_grad = both(w_q_grad, qa_rows, 0)
         qb_rows = tn_dot(n_half, dq_b)
-        w_q_grad = both(w_q_grad, qb_rows, cut).reshape(width, heads_width)
+        w_q_grad = put(put(w_q_grad, qa_rows, core, 0), qb_rows, core, cut)
+        for rows, col in ((qa_rows, 0), (qb_rows, cut)):
+            w_q_grad = put(w_q_grad, swap(rows, 1), 1 - core, col)
+        w_q_grad = w_q_grad.reshape(width, heads_width)
         return (block_out[None], x_grad[None], small[0], w_q_grad, w_k_grad, w_v_grad, w_o_grad, small[1])
 
     return jax.shard_map(step, mesh=mesh,

time: 931 us -> 933 us (level)
    unnamed x61 -> x65, local copies, waits for them, and re-layouts: 7.8 us -> 23.2 us
  transfers between devices with their start and end apart: 43 -> 43, of which waited for: 13 -> 13; matrix products, arithmetic and copies ran while one was open for 43% -> 42% of each run, Pallas kernels for 7% -> 7%
where the time goes in v1:
time: 933 us; the launch traced here: 925 us
  waiting for transfers between devices  315 us (34%)
  matrix products  275 us (29%)
  local copies, waits for them, and re-layouts  123 us (13%)
  starting transfers between devices  94.5 us (10%)
  Pallas kernels  64 us (7%)
  other arithmetic  39.4 us (4%)
  between operations  14.6 us (2%)
    dot_general x4, matrix products, tn_dot(): lax.dot_general(a, b, (((0,), (0,)), ((), ())), preferred_element_type=f32)  162 us
    all_gather x3, waiting for transfers between devices, gather(): return lax.all_gather(a, 'sp', axis=0, tiled=True)  141 us
    ppermute x38, waiting for transfers between devices, swap(): return lax.ppermute(a, 'sp', [(i, i ^ bit) for i in range(n_sp)])  114 us
    ppermute x38, starting transfers between devices, swap(): return lax.ppermute(a, 'sp', [(i, i ^ bit) for i in range(n_sp)])  94.3 us
    pallas_call x1, Pallas kernels, attention(): pl.pallas_call(attention_kernel, out_shape=(jax.ShapeDtypeStruct((tokens,...  64 us
    all_gather x2, waiting for transfers between devices, gather_chips(): return lax.all_gather(a, 'sp', axis=0, tiled=True, axis_index_groups=groups)  59.1 us
    dot_general x4, matrix products, nt_dot(): lax.dot_general(a, b, (((1,), (1,)), ((), ())), preferred_element_type=jn...  58.3 us
    dot_general x4, matrix products, nn_dot(): lax.dot_general(a, b, (((1,), (0,)), ((), ())), preferred_element_type=jn...  54.7 us
  transfers between devices with their start and end apart: 43, of which 13 were waited for; matrix products, arithmetic and copies ran while one was open for 42% of the time, Pallas kernels for 7%

profile of v1, /device:TPU:11, one launch (start us, length us, event | category | flops | bytes accessed | tf_op | source)
XLA Modules:
  0.0 925.1 jit_solution(3640146529337577377)
XLA Ops:
  7.2 3.0 fusion.10
  11.5 5.1 fusion.7
  16.6 3.5 broadcast_select_fusion.1
  20.7 2.1 broadcast_in_dim.73
  25.8 2.9 bitcast_dynamic-update-slice_fusion.10
  30.3 3.7 fusion.48
  36.3 3.9 convolution_convert_fusion.4
  44.4 23.6 %fusion.47.q_ref = f32[512,4096]{1,0:T(8,128)} fusion(bf16[512,3584]{1,0:T(8,128)(2,1)S(1)} %copy-done.3, bf16[3584,4096]{1,0:T(8,128)(2,1)} %param.15), kind=kOutput, calls=%fused_computation.137 | convolution fusion | flops 15032385536 | bytes 41418752 | tf_op jit(solution)/shard_map/dot_general | solution.py:35
  68.0 22.6 %convolution_convert_fusion.1.do_ref = bf16[512,4096]{1,0:T(8,128)(2,1)} fusion(bf16[4096,3584]{1,0:T(8,128)(2,1)} %param.18, bf16[1,512,3584]{2,1,0:T(8,128)(2,1)S(1)} %copy-done.9), kind=kOutput, calls=%fused_computation.29 | convolution fusion | flops 15034482688 | bytes 37224448 | tf_op jit(solution)/shard_map/dot_general | solution.py:31
  100.4 22.5 %collective-permute-done.11 = bf16[512,512]{1,0:T(8,128)(2,1)} collective-permute-done((bf16[512,512]{1,0:T(8,128)(2,1)}, bf16[512,512]{1,0:T(8,128)(2,1)}, u32[]{:S(2)}, u32[]{:S(2)}) %collective-permute-start.11) | collective-permute-done | bytes 524320 | tf_op jit(solution)/shard_map/ppermute | solution.py:230
  129.5 8.1 collective-permute-done.13
  138.6 2.1 collective-permute-start.15
  146.7 64.0 %shard_map.161 = (bf16[512,4096]{1,0:T(8,128)(2,1)}, bf16[512,4096]{1,0:T(8,128)(2,1)}, f32[4096,512]{1,0:T(8,128)}) custom-call(s32[2]{0:T(128)} %and_select_fusion.first_blk, s32[1]{0:T(128)} %bitcast.3.base_blk, f32[512,4096]{1,0:T(8,128)} %fusion.47.q_ref, bf16[512,4096]{1,0:T(8,128)(2,1)} %convolution_convert_fusion.1.do_ref, ...), custom_call_target="tpu_custom_call" | custom-call | flops 51539607552 | bytes 33554432 | tf_op jit(solution)/shard_map/pallas_call | solution.py:179
  210.8 3.7 slice.117
  214.6 2.6 broadcast_select_fusion
  217.2 2.5 broadcast_in_dim.83
  219.7 2.1 bitcast_dynamic-update-slice_fusion.7
  224.0 4.7 dynamic-slice_bitcast_fusion
  229.1 7.1 collective-permute-done.16
  236.2 4.5 bitcast_add_fusion
  244.8 65.1 %collective-permute-start.19 = (f32[2,256,512]{2,1,0:T(8,128)}, f32[2,256,512]{2,1,0:T(8,128)}, u32[]{:S(2)}, u32[]{:S(2)}) collective-permute-start(f32[2,256,512]{2,1,0:T(8,128)} %dynamic-slice_bitcast_fusion.1), channel_id=1, source_target_pairs={{0,4},{1,5},{2,6},{3,7},{4,0},{5,1},{6,2},{7,3},{8,12},{9,13},{10,... | collective-permute-start | bytes 3145736 | tf_op jit(solution)/shard_map/ppermute | solution.py:230
  309.9 2.3 dynamic-slice_bitcast_fusion.2
  312.2 34.2 %collective-permute-done.19 = f32[2,256,512]{2,1,0:T(8,128)} collective-permute-done((f32[2,256,512]{2,1,0:T(8,128)}, f32[2,256,512]{2,1,0:T(8,128)}, u32[]{:S(2)}, u32[]{:S(2)}) %collective-permute-start.19) | collective-permute-done | bytes 1048608 | tf_op jit(solution)/shard_map/ppermute | solution.py:230
  350.0 18.7 %collective-permute-done.20 = f32[256,512]{1,0:T(8,128)S(1)} collective-permute-done((f32[256,512]{1,0:T(8,128)S(1)}, f32[256,512]{1,0:T(8,128)S(1)}, u32[]{:S(2)}, u32[]{:S(2)}) %collective-permute-start.20) | collective-permute-done | bytes 524320 | tf_op jit(solution)/shard_map/ppermute | solution.py:230
  368.7 2.1 collective-permute-done.18
  371.4 4.2 fusion.24
  375.7 4.2 fusion.32
  379.9 27.3 %fusion.9 = (f32[3584]{0:T(1024)S(1)}, f32[512]{0:T(512)S(1)}, bf16[512,3584]{1,0:T(8,128)(2,1)}) fusion(bf16[1,512,3584]{2,1,0:T(8,128)(2,1)S(1)} %copy-done.4, f32[512]{0:T(512)S(1)} %copy-done.22, f32[3584]{0:T(1024)S(1)} %copy-done.18, f32[512,3584]{1,0:T(8,128)} %fusion.24, f32[512,3584]{1,0:T(8,128)} %fusion.32, ...), kind=kOutput, calls=%fused_computation.23 | convolution fusion | flops 15052566528 | bytes 55607296 | tf_op jit(solution)/shard_map/dot_general | solution.py:31
  407.2 6.4 convert_reduce_fusion
  413.7 2.9 collective-permute-start.21
  419.2 2.6 collective-permute-start.28
  421.9 2.3 slice.118
  424.8 17.4 %collective-permute-done.30 = bf16[512,512]{1,0:T(8,128)(2,1)S(1)} collective-permute-done((bf16[512,512]{1,0:T(8,128)(2,1)S(1)}, bf16[512,512]{1,0:T(8,128)(2,1)S(1)}, u32[]{:S(2)}, u32[]{:S(2)}) %collective-permute-start.30) | collective-permute-done | bytes 524320 | tf_op jit(solution)/shard_map/ppermute | solution.py:230
  457.9 14.0 %convolution_convert_fusion.3 = bf16[1792,512]{1,0:T(8,128)(2,1)} fusion(bf16[4096,1792]{1,0:T(8,128)(2,1)} %all-gather.7.cloned.1.call-done, bf16[4096,512]{1,0:T(8,128)(2,1)} %constant_dynamic-update-slice_fusion.5), kind=kOutput, calls=%fused_computation.38 | convolution fusion | flops 7517110272 | bytes 20709376 | tf_op jit(solution)/shard_map/dot_general | solution.py:220
  472.1 14.0 %broadcast_in_dim.69 = bf16[2,1792,4096]{2,1,0:T(8,128)(2,1)} broadcast(bf16[]{:T(256)} %constant.103.clone.1), dimensions={} | broadcast | bytes 29360130 | tf_op jit(solution)/shard_map/broadcast_in_dim | solution.py:307
  486.5 52.5 %bitcast_dynamic-update-slice_fusion.3 = (bf16[2,1792,4096]{2,1,0:T(8,128)(2,1)}, bf16[1792,3072]{1,0:T(8,128)(2,1)}) fusion(bf16[2,1792,4096]{2,1,0:T(8,128)(2,1)} %broadcast_in_dim.69, s32[]{:T(128)S(6)} %select_n.122, bf16[4096,1792]{1,0:T(8,128)(2,1)S(1)} %copy-done.26, bf16[4096,3072]{1,0:T(8,128)(2,1)} %all-gather.9.cloned.1.call-done), kind=kOutput, calls=%fused_computation.12 | convolution fusion | flops 45102661632 | bytes 61865988 | tf_op jit(solution)/shard_map/dot_general | solution.py:220
  539.3 59.1 %all-gather.13.cloned.1.call-done = bf16[4096,2048]{1,0:T(8,128)(2,1)} async-done(((bf16[1024,2048]{1,0:T(8,128)(2,1)}), bf16[4096,2048]{1,0:T(8,128)(2,1)}) %all-gather.13.cloned.1.call-update) | async-done | bytes 16777232 | tf_op jit(solution)/shard_map/all_gather | solution.py:227
  598.5 141.5 %all-gather.15.cloned.1.call-done = bf16[1,4096,3584]{2,1,0:T(8,128)(2,1)} async-done(((bf16[1,512,3584]{2,1,0:T(8,128)(2,1)}), bf16[1,4096,3584]{2,1,0:T(8,128)(2,1)}) %all-gather.15.cloned.1.call-update) | async-done | bytes 29360144 | tf_op jit(solution)/shard_map/all_gather | solution.py:223
  739.9 71.6 %fusion.2 = bf16[2048,3584]{1,0:T(8,128)(2,1)} fusion(bf16[4096,2048]{1,0:T(8,128)(2,1)} %all-gather.13.cloned.1.call-done, bf16[1,4096,3584]{2,1,0:T(8,128)(2,1)} %all-gather.15.cloned.1.call-done), kind=kOutput, calls=%fused_computation.2 | convolution fusion | flops 60136882176 | bytes 60817408 | tf_op jit(solution)/shard_map/dot_general | solution.py:220
  811.8 23.5 %fusion.14 = bf16[1,512,3584]{2,1,0:T(8,128)(2,1)} fusion(bf16[512,4096]{1,0:T(8,128)(2,1)} %get-tuple-element.15, bf16[4096,3584]{1,0:T(8,128)(2,1)} %param.18, bf16[1,512,3584]{2,1,0:T(8,128)(2,1)S(1)} %copy-done.5, f32[3584]{0:T(1024)S(1)} %convert_element_type.80), kind=kOutput, calls=%fused_computation.30 | convolution fusion | flops 15039725568 | bytes 40908800 | tf_op jit(solution)/shard_map/dot_general | solution.py:35
  842.5 23.4 %bitcast_dynamic-update-slice_fusion.5 = (bf16[2,1792,4096]{2,1,0:T(8,128)(2,1)}, bf16[1792,1024]{1,0:T(8,128)(2,1)}) fusion(bf16[2,1792,4096]{2,1,0:T(8,128)(2,1)} %get-tuple-element.45, s32[]{:T(128)S(6)} %select_n.122, bf16[4096,1792]{1,0:T(8,128)(2,1)} %all-gather.7.cloned.1.call-done, bf16[4096,1024]{1,0:T(8,128)(2,1)} %all-gather.11.cloned.1.call-done), kind=kOutput, calls=%fused_computation.36 | convolution fusion | flops 15034220544 | bytes 30408708 | tf_op jit(solution)/shard_map/dot_general | solution.py:220
  866.1 10.1 %broadcast_in_dim.68 = bf16[2,2048,3584]{2,1,0:T(8,128)(2,1)} broadcast(bf16[]{:T(256)} %constant.103.clone.1), dimensions={} | broadcast | bytes 29360130 | tf_op jit(solution)/shard_map/broadcast_in_dim | solution.py:307
  876.2 5.9 bitcast_dynamic-update-slice_fusion.1
  882.1 10.5 %bitcast_dynamic-update-slice_fusion.2 = bf16[2,1792,4096]{2,1,0:T(8,128)(2,1)} fusion(bf16[2,1792,4096]{2,1,0:T(8,128)(2,1)} %get-tuple-element.47, s32[]{:T(128)S(6)} %select_n.123, bf16[1792,3072]{1,0:T(8,128)(2,1)} %collective-permute-done.25), kind=kLoop, calls=%fused_computation.11 | loop fusion | bytes 22020100 | tf_op jit(solution)/shard_map/dynamic_update_slice | solution.py:276
  892.6 2.3 bitcast_dynamic-update-slice_fusion.4
  894.9 5.2 copy-done.6
  900.1 7.9 bitcast_dynamic-update-slice_fusion
  908.0 10.3 %copy-done.7 = bf16[2,2048,3584]{2,1,0:T(8,128)(2,1)} copy-done((bf16[2,2048,3584]{2,1,0:T(8,128)(2,1)}, bf16[2,2048,3584]{2,1,0:T(8,128)(2,1)S(1)}, u32[]{:S(2)}) %copy-start.7) | copy-done | bytes 29360152
  (221 shorter events, 74.8 us)
Async XLA Ops:
  7.2 450.7 %all-gather.7.cloned.1.call-start = ((), (), s32[]{:S(2)}) async-start(), calls=%async_computation | async-start | bytes 18350080 | tf_op jit(solution)/shard_map/all_gather | solution.py:227
  20.1 5.7 collective-permute-start.24
  28.7 443.4 %all-gather.9.cloned.1.call-start = ((), (), s32[]{:S(2)}) async-start(), calls=%async_computation.1 | async-start | bytes 28311552 | tf_op jit(solution)/shard_map/all_gather | solution.py:223
  28.7 67.8 %collective-permute-start = (s32[512]{0:T(512)S(1)}, s32[512]{0:T(512)S(1)}, u32[]{:S(2)}, u32[]{:S(2)}) collective-permute-start(s32[512]{0:T(512)S(1)} %bitcast.111), channel_id=1, source_target_pairs={{0,1},{1,0},{2,3},{3,2},{4,5},{5,4},{6,7},{7,6},{8,9},{9,8},{10,11... | collective-permute-start | bytes 6152 | tf_op jit(solution)/shard_map/ppermute | solution.py:230
  28.8 62.9 %collective-permute-start.1 = (s32[512]{0:T(512)S(1)}, s32[512]{0:T(512)S(1)}, u32[]{:S(2)}, u32[]{:S(2)}) collective-permute-start(s32[512]{0:T(512)S(1)} %bitcast.112), channel_id=1, source_target_pairs={{0,2},{1,3},{2,0},{3,1},{4,6},{5,7},{6,4},{7,5},{8,10},{9,11},{10,... | collective-permute-start | bytes 6152 | tf_op jit(solution)/shard_map/ppermute | solution.py:230
  29.1 61.5 %collective-permute-start.3 = (s32[512]{0:T(512)S(1)}, s32[512]{0:T(512)S(1)}, u32[]{:S(2)}, u32[]{:S(2)}) collective-permute-start(s32[512]{0:T(512)S(1)} %bitcast.113), channel_id=1, source_target_pairs={{0,4},{1,5},{2,6},{3,7},{4,0},{5,1},{6,2},{7,3},{8,12},{9,13},{10,... | collective-permute-start | bytes 6152 | tf_op jit(solution)/shard_map/ppermute | solution.py:230
  43.5 84.1 %collective-permute-start.8 = (bf16[512,512]{1,0:T(8,128)(2,1)}, bf16[512,512]{1,0:T(8,128)(2,1)}, u32[]{:S(2)}, u32[]{:S(2)}) collective-permute-start(bf16[512,512]{1,0:T(8,128)(2,1)} %get-tuple-element.36), channel_id=1, source_target_pairs={{0,1},{1,0},{2,3},{3,2},{4,5},{5,4},{6,7},{7,6},{8,9},{9,8},{10,11... | collective-permute-start | bytes 1572872 | tf_op jit(solution)/shard_map/ppermute | solution.py:230
  90.6 3.0 collective-permute-start.5
  91.6 3.4 collective-permute-start.6
  92.1 5.5 collective-permute-start.2
  93.5 4.6 collective-permute-start.4
  95.1 3.5 collective-permute-start.7
  96.6 28.3 %collective-permute-start.9 = (bf16[512,512]{1,0:T(8,128)(2,1)}, bf16[512,512]{1,0:T(8,128)(2,1)S(1)}, u32[]{:S(2)}, u32[]{:S(2)}) collective-permute-start(bf16[512,512]{1,0:T(8,128)(2,1)} %get-tuple-element.36), channel_id=1, source_target_pairs={{0,2},{1,3},{2,0},{3,1},{4,6},{5,7},{6,4},{7,5},{8,10},{9,11},{10,... | collective-permute-start | bytes 1572872 | tf_op jit(solution)/shard_map/ppermute | solution.py:230
  97.6 25.4 %collective-permute-start.11 = (bf16[512,512]{1,0:T(8,128)(2,1)}, bf16[512,512]{1,0:T(8,128)(2,1)}, u32[]{:S(2)}, u32[]{:S(2)}) collective-permute-start(bf16[512,512]{1,0:T(8,128)(2,1)} %get-tuple-element.36), channel_id=1, source_target_pairs={{0,4},{1,5},{2,6},{3,7},{4,0},{5,1},{6,2},{7,3},{8,12},{9,13},{10,... | collective-permute-start | bytes 1572872 | tf_op jit(solution)/shard_map/ppermute | solution.py:230
  100.3 45.6 %copy-start.16 = (s32[512,1]{1,0:T(8,128)}, s32[512,1]{1,0:T(8,128)S(1)}, u32[]{:S(2)}) copy-start(s32[512,1]{1,0:T(8,128)S(1)} %add_maximum_fusion.low_ref) | copy-start | bytes 6148
  123.9 13.7 %collective-permute-start.13 = (bf16[256,512]{1,0:T(8,128)(2,1)S(1)}, bf16[256,512]{1,0:T(8,128)(2,1)S(1)}, u32[]{:S(2)}, u32[]{:S(2)}) collective-permute-start(bf16[256,512]{1,0:T(8,128)(2,1)S(1)} %slice.131), channel_id=1, source_target_pairs={{0,2},{1,3},{2,0},{3,1},{4,6},{5,7},{6,4},{7,5},{8,10},{9,11},{10,... | collective-permute-start | bytes 786440 | tf_op jit(solution)/shard_map/ppermute | solution.py:230
  124.9 13.6 %collective-permute-start.14 = (bf16[256,512]{1,0:T(8,128)(2,1)S(1)}, bf16[256,512]{1,0:T(8,128)(2,1)S(1)}, u32[]{:S(2)}, u32[]{:S(2)}) collective-permute-start(bf16[256,512]{1,0:T(8,128)(2,1)S(1)} %slice.132), channel_id=1, source_target_pairs={{0,4},{1,5},{2,6},{3,7},{4,0},{5,1},{6,2},{7,3},{8,12},{9,13},{10,... | collective-permute-start | bytes 786440 | tf_op jit(solution)/shard_map/ppermute | solution.py:230
  125.4 16.1 %collective-permute-start.10 = (bf16[512,512]{1,0:T(8,128)(2,1)S(1)}, bf16[512,512]{1,0:T(8,128)(2,1)S(1)}, u32[]{:S(2)}, u32[]{:S(2)}) collective-permute-start(bf16[512,512]{1,0:T(8,128)(2,1)S(1)} %collective-permute-done.9), channel_id=1, source_target_pairs={{0,1},{1,0},{2,3},{3,2},{4,5},{5,4},{6,7},{7,6},{8,9},{9,8},{10,11... | collective-permute-start | bytes 1572872 | tf_op jit(solution)/shard_map/ppermute | solution.py:230
  127.6 16.6 %collective-permute-start.12 = (bf16[512,512]{1,0:T(8,128)(2,1)}, bf16[512,512]{1,0:T(8,128)(2,1)S(1)}, u32[]{:S(2)}, u32[]{:S(2)}) collective-permute-start(bf16[512,512]{1,0:T(8,128)(2,1)} %collective-permute-done.11), channel_id=1, source_target_pairs={{0,1},{1,0},{2,3},{3,2},{4,5},{5,4},{6,7},{7,6},{8,9},{9,8},{10,11... | collective-permute-start | bytes 1572872 | tf_op jit(solution)/shard_map/ppermute | solution.py:230
  138.6 7.3 collective-permute-start.15
  214.5 383.9 %all-gather.13.cloned.1.call-start = ((), (), s32[]{:S(2)}) async-start(), calls=%async_computation.3 | async-start | bytes 20971520 | tf_op jit(solution)/shard_map/all_gather | solution.py:227
  217.2 4.7 collective-permute-start.36
  223.3 516.6 %all-gather.15.cloned.1.call-start = ((), (), s32[]{:S(2)}) async-start(), calls=%async_computation.4 | async-start | bytes 33030144 | tf_op jit(solution)/shard_map/all_gather | solution.py:223
  223.9 618.5 %all-gather.11.cloned.1.call-start = ((), (), s32[]{:S(2)}) async-start(), calls=%async_computation.2 | async-start | bytes 9437184 | tf_op jit(solution)/shard_map/all_gather | solution.py:223
  228.6 7.6 collective-permute-start.16
  244.8 101.5 %collective-permute-start.19 = (f32[2,256,512]{2,1,0:T(8,128)}, f32[2,256,512]{2,1,0:T(8,128)}, u32[]{:S(2)}, u32[]{:S(2)}) collective-permute-start(f32[2,256,512]{2,1,0:T(8,128)} %dynamic-slice_bitcast_fusion.1), channel_id=1, source_target_pairs={{0,4},{1,5},{2,6},{3,7},{4,0},{5,1},{6,2},{7,3},{8,12},{9,13},{10,... | collective-permute-start | bytes 3145736 | tf_op jit(solution)/shard_map/ppermute | solution.py:230
  312.2 36.1 %collective-permute-start.17 = (f32[2,256,512]{2,1,0:T(8,128)}, f32[2,256,512]{2,1,0:T(8,128)}, u32[]{:S(2)}, u32[]{:S(2)}) collective-permute-start(f32[2,256,512]{2,1,0:T(8,128)} %dynamic-slice_bitcast_fusion.2), channel_id=1, source_target_pairs={{0,2},{1,3},{2,0},{3,1},{4,6},{5,7},{6,4},{7,5},{8,10},{9,11},{10,... | collective-permute-start | bytes 3145736 | tf_op jit(solution)/shard_map/ppermute | solution.py:230
  312.2 36.1 %copy-start.10 = (f32[2,2,256,512]{3,2,1,0:T(8,128)S(1)}, f32[2,2,256,512]{3,2,1,0:T(8,128)}, u32[]{:S(2)}) copy-start(f32[2,2,256,512]{3,2,1,0:T(8,128)} %get-tuple-element.29) | copy-start | bytes 6291460
  348.2 20.4 %collective-permute-start.20 = (f32[256,512]{1,0:T(8,128)S(1)}, f32[256,512]{1,0:T(8,128)S(1)}, u32[]{:S(2)}, u32[]{:S(2)}) collective-permute-start(f32[256,512]{1,0:T(8,128)S(1)} %dynamic-slice_bitcast_fusion.3), channel_id=1, source_target_pairs={{0,2},{1,3},{2,0},{3,1},{4,6},{5,7},{6,4},{7,5},{8,10},{9,11},{10,... | collective-permute-start | bytes 1572872 | tf_op jit(solution)/shard_map/ppermute | solution.py:230
  349.8 21.1 %collective-permute-start.18 = (f32[256,512]{1,0:T(8,128)S(1)}, f32[256,512]{1,0:T(8,128)S(1)}, u32[]{:S(2)}, u32[]{:S(2)}) collective-permute-start(f32[256,512]{1,0:T(8,128)S(1)} %dynamic-slice_bitcast_fusion.4), channel_id=1, source_target_pairs={{0,4},{1,5},{2,6},{3,7},{4,0},{5,1},{6,2},{7,3},{8,12},{9,13},{10,... | collective-permute-start | bytes 1572872 | tf_op jit(solution)/shard_map/ppermute | solution.py:230
  413.7 8.2 collective-permute-start.21
  419.0 23.3 %collective-permute-start.30 = (bf16[512,512]{1,0:T(8,128)(2,1)S(1)}, bf16[512,512]{1,0:T(8,128)(2,1)S(1)}, u32[]{:S(2)}, u32[]{:S(2)}) collective-permute-start(bf16[512,512]{1,0:T(8,128)(2,1)S(1)} %get-tuple-element.25), channel_id=1, source_target_pairs={{0,4},{1,5},{2,6},{3,7},{4,0},{5,1},{6,2},{7,3},{8,12},{9,13},{10,... | collective-permute-start | bytes 1572872 | tf_op jit(solution)/shard_map/ppermute | solution.py:230
  419.2 24.6 %collective-permute-start.28 = (bf16[512,512]{1,0:T(8,128)(2,1)S(1)}, bf16[512,512]{1,0:T(8,128)(2,1)S(1)}, u32[]{:S(2)}, u32[]{:S(2)}) collective-permute-start(bf16[512,512]{1,0:T(8,128)(2,1)S(1)} %get-tuple-element.25), channel_id=1, source_target_pairs={{0,2},{1,3},{2,0},{3,1},{4,6},{5,7},{6,4},{7,5},{8,10},{9,11},{10,... | collective-permute-start | bytes 1572872 | tf_op jit(solution)/shard_map/ppermute | solution.py:230
  421.9 23.2 %collective-permute-start.22 = (f32[2,3584]{1,0:T(2,128)S(1)}, f32[2,3584]{1,0:T(2,128)S(1)}, u32[]{:S(2)}, u32[]{:S(2)}) collective-permute-start(f32[2,3584]{1,0:T(2,128)S(1)} %fusion.41), channel_id=1, source_target_pairs={{0,2},{1,3},{2,0},{3,1},{4,6},{5,7},{6,4},{7,5},{8,10},{9,11},{10,... | collective-permute-start | bytes 86024 | tf_op jit(solution)/shard_map/ppermute | solution.py:230
  424.2 22.8 %collective-permute-start.27 = (bf16[512,512]{1,0:T(8,128)(2,1)S(1)}, bf16[512,512]{1,0:T(8,128)(2,1)S(1)}, u32[]{:S(2)}, u32[]{:S(2)}) collective-permute-start(bf16[512,512]{1,0:T(8,128)(2,1)S(1)} %get-tuple-element.25), channel_id=1, source_target_pairs={{0,1},{1,0},{2,3},{3,2},{4,5},{5,4},{6,7},{7,6},{8,9},{9,8},{10,11... | collective-permute-start | bytes 1572872 | tf_op jit(solution)/shard_map/ppermute | solution.py:230
  442.3 7.4 collective-permute-start.32
  443.8 7.1 collective-permute-start.33
  444.0 9.7 %collective-permute-start.29 = (bf16[512,512]{1,0:T(8,128)(2,1)S(1)}, bf16[512,512]{1,0:T(8,128)(2,1)S(1)}, u32[]{:S(2)}, u32[]{:S(2)}) collective-permute-start(bf16[512,512]{1,0:T(8,128)(2,1)S(1)} %collective-permute-done.28), channel_id=1, source_target_pairs={{0,1},{1,0},{2,3},{3,2},{4,5},{5,4},{6,7},{7,6},{8,9},{9,8},{10,11... | collective-permute-start | bytes 1572872 | tf_op jit(solution)/shard_map/ppermute | solution.py:230
  445.7 389.5 %collective-permute-start.23 = (f32[2,3584]{1,0:T(2,128)}, f32[2,3584]{1,0:T(2,128)}, u32[]{:S(2)}, u32[]{:S(2)}) collective-permute-start(f32[2,3584]{1,0:T(2,128)} %fusion.69), channel_id=1, source_target_pairs={{0,4},{1,5},{2,6},{3,7},{4,0},{5,1},{6,2},{7,3},{8,12},{9,13},{10,... | collective-permute-start | bytes 86024 | tf_op jit(solution)/shard_map/ppermute | solution.py:230
  447.0 8.4 collective-permute-start.31
  450.9 6.1 collective-permute-start.34
  471.9 366.8 %collective-permute-start.35 = (bf16[1792,512]{1,0:T(8,128)(2,1)}, bf16[1792,512]{1,0:T(8,128)(2,1)}, u32[]{:S(2)}, u32[]{:S(2)}) collective-permute-start(bf16[1792,512]{1,0:T(8,128)(2,1)} %convolution_convert_fusion.3), channel_id=1, source_target_pairs={{0,1},{1,0},{2,3},{3,2},{4,5},{5,4},{6,7},{7,6},{8,9},{9,8},{10,11... | collective-permute-start | bytes 5505032 | tf_op jit(solution)/shard_map/ppermute | solution.py:230
  539.0 343.1 %collective-permute-start.25 = (bf16[1792,3072]{1,0:T(8,128)(2,1)}, bf16[1792,3072]{1,0:T(8,128)(2,1)}, u32[]{:S(2)}, u32[]{:S(2)}) collective-permute-start(bf16[1792,3072]{1,0:T(8,128)(2,1)} %get-tuple-element.46), channel_id=1, source_target_pairs={{0,1},{1,0},{2,3},{3,2},{4,5},{5,4},{6,7},{7,6},{8,9},{9,8},{10,11... | collective-permute-start | bytes 33030152 | tf_op jit(solution)/shard_map/ppermute | solution.py:230
  739.9 71.9 %copy-start.5 = (bf16[1,512,3584]{2,1,0:T(8,128)(2,1)S(1)}, bf16[1,512,3584]{2,1,0:T(8,128)(2,1)}, u32[]{:S(2)}) copy-start(bf16[1,512,3584]{2,1,0:T(8,128)(2,1)} %param.10) | copy-start | bytes 11010052
  811.6 83.3 %collective-permute-start.37 = (bf16[2048,3584]{1,0:T(8,128)(2,1)}, bf16[2048,3584]{1,0:T(8,128)(2,1)}, u32[]{:S(2)}, u32[]{:S(2)}) collective-permute-start(bf16[2048,3584]{1,0:T(8,128)(2,1)} %fusion.2), channel_id=1, source_target_pairs={{0,1},{1,0},{2,3},{3,2},{4,5},{5,4},{6,7},{7,6},{8,9},{9,8},{10,11... | collective-permute-start | bytes 44040200 | tf_op jit(solution)/shard_map/ppermute | solution.py:230
  842.4 33.8 %slice-start.1 = ((s8[14680064]{0:T(1024)(128)(4,1)}), s8[4194304]{0:T(1024)(128)(4,1)S(1)}, s32[]{:S(2)}) async-start(s8[14680064]{0:T(1024)(128)(4,1)} %bitcast.105), calls=%async_computation.6 | async-start | bytes 8388608
  842.5 33.8 %slice-start.2 = ((s8[14680064]{0:T(1024)(128)(4,1)}), s8[4194304]{0:T(1024)(128)(4,1)S(1)}, s32[]{:S(2)}) async-start(s8[14680064]{0:T(1024)(128)(4,1)} %bitcast.105), calls=%async_computation.7 | async-start | bytes 8388608
  865.8 26.8 %collective-permute-start.26 = (bf16[1792,1024]{1,0:T(8,128)(2,1)}, bf16[1792,1024]{1,0:T(8,128)(2,1)S(1)}, u32[]{:S(2)}, u32[]{:S(2)}) collective-permute-start(bf16[1792,1024]{1,0:T(8,128)(2,1)} %get-tuple-element.48), channel_id=1, source_target_pairs={{0,1},{1,0},{2,3},{3,2},{4,5},{5,4},{6,7},{7,6},{8,9},{9,8},{10,11... | collective-permute-start | bytes 11010056 | tf_op jit(solution)/shard_map/ppermute | solution.py:230
  (26 other events, 278.2 us)
Sparse Core Ops, SparseCore 0:
  28.8 153.2 all-gather.6
  214.6 228.9 all-gather.8
  445.5 152.9 all-gather.12
  600.1 139.7 all-gather.14
  741.6 50.4 all-gather.10
